TPU v7x, 8 devices: a whole 2x2x1 slice. The times are simulated.
8 devices in a mesh: dp: 2 (over z, y), sp: 4 (over x, core).
Axes of the slice: x: 2, y: 2, z: 1, core: 2. Of those that a mesh axis runs over, the one named last changes fastest.
Arguments:
- images: float32 [64, 512, 512, 3], P('dp', 'sp'), parts along dimension 0
- w_patch: bfloat16 [16, 16, 3, 1152], replicated
- b_patch: float32 [1152], replicated
- pos_embed: bfloat16 [1024, 1152], P('sp')
- ln1_gain: float32 [1152], replicated
- ln1_bias: float32 [1152], replicated
- w_qkv: bfloat16 [1152, 3, 16, 72], replicated
- b_qkv: float32 [3, 16, 72], replicated
- w_out: bfloat16 [16, 72, 1152], replicated
- b_out: float32 [1152], replicated
- ln2_gain: float32 [1152], replicated
- ln2_bias: float32 [1152], replicated
- w_fc1: bfloat16 [1152, 4304], replicated
- b_fc1: float32 [4304], replicated
- w_fc2: bfloat16 [4304, 1152], replicated
- b_fc2: float32 [1152], replicated
Outputs:
- output: bfloat16 [64, 1024, 1152], P('dp', 'sp'), parts along dimension 0
There are 2 independent parts. A program takes and returns all parts, laid end to end along the dimension named above; an argument that names none is the same for every part.
All inputs are finite; a program needn't handle non-finite values.
Results may differ from a plain program's by a relative error of at most 0.00841065.
Values are sent between devices in bfloat16 or wider.
A program may use at most 1 GiB of HBM per device.

v0:
```python
import functools
import jax
import jax.numpy as jnp
from jax import lax
from jax.experimental import pallas as pl
from jax.experimental.pallas import tpu as pltpu
from jax.sharding import PartitionSpec as P


LN_EPS = 1e-6
GROUPS = (2, 6)
CHUNKS = (2, 3, 2, 1)
DOWN = 512
MIB = 2 ** 20
F32, BF16 = jnp.float32, jnp.bfloat16


def dot(a, b):
    return jnp.dot(a, b, preferred_element_type=F32)


def widen(col, lanes):
    return jnp.concatenate([col] * (lanes // 128), axis=1)


def embed_kernel(idx_ref, i0, i1, i2, i3, perm_ref, wp_ref, bp_ref, pos_ref, o0, o1, o2, o3, xs):
    imgs = (i0, i1, i2, i3)
    outs = (o0, o1, o2, o3)
    zs = []
    for j in range(4):
        rows = []
        for k in range(4):
            for g in range(2):
                y = (4 * g + j) * 16
                for c in range(3):
                    rows.append(imgs[k][0, c, y:y + 16, :])
        zs.append(dot(jnp.concatenate(rows, axis=0).astype(BF16), perm_ref[j]))
    group = lax.broadcasted_iota(jnp.int32, (48, 128), 1) // 32
    for k in range(4):
        for g in range(2):
            r = (k * 2 + g) * 48
            for v in range(4):
                for u in range(4):
                    acc = zs[0][r:r + 48, 128 * v:128 * v + 128]
                    for j in range(1, 4):
                        acc = jnp.where(group == (u + j) % 4, zs[j][r:r + 48, 128 * v:128 * v + 128], acc)
                    if u:
                        acc = pltpu.roll(acc, 128 - 32 * u, 1)
                    px = 4 * v + u
                    xs[px * 48:px * 48 + 48, k * 256 + g * 128:k * 256 + g * 128 + 128] = acc.astype(BF16)
    step = 384

    def body(m, _):
        ms = pl.multiple_of(m * step, step)
        t = dot(wp_ref[pl.ds(ms, step), :], xs[...])
        t = t + widen(bp_ref[pl.ds(ms, step), :], 1024)
        p = pos_ref[pl.ds(ms, step), :].astype(F32)
        t = (t + jnp.concatenate([p] * 4, axis=1)).astype(BF16)
        for k in range(4):
            outs[k][0, pl.ds(ms, step), :] = t[:, k * 256:(k + 1) * 256]
        return 0

    lax.fori_loop(0, 1152 // step, body, 0)


def embed(idx, planes, perm, wp, bp, pos, n):
    d = wp.shape[0]

    def img(k):
        return pl.BlockSpec((1, 3, 128, 512), lambda i, idx, k=k: (idx[k] + i, 0, 0, 0))

    def whole(a):
        return pl.BlockSpec(a.shape, lambda i, idx: (0,) * a.ndim, pipeline_mode=pl.Buffered(1))

    return pl.pallas_call(
        embed_kernel,
        grid_spec=pltpu.PrefetchScalarGridSpec(
            num_scalar_prefetch=1, grid=(n,),
            in_specs=[img(0), img(1), img(2), img(3), whole(perm), whole(wp), whole(bp), whole(pos)],
            out_specs=[pl.BlockSpec((1, d, 256), lambda i, idx: (i, 0, 0))] * 4,
            scratch_shapes=[pltpu.VMEM((768, 1024), BF16)]),
        out_shape=[jax.ShapeDtypeStruct((n, d, 256), BF16)] * 4,
        name="embed",
        cost_estimate=pl.CostEstimate(flops=2 * n * 1024 * 768 * 1152, bytes_accessed=n * 6 * MIB, transcendentals=0),
        compiler_params=pltpu.CompilerParams(vmem_limit_bytes=56 * MIB),
    )(idx, planes, planes, planes, planes, perm, wp, bp, pos)


def row_mean(x, parts=8):
    rows = x.shape[0] // parts
    sums = [jnp.sum(x[i * rows:(i + 1) * rows].reshape(rows // 8, 8, x.shape[1]), axis=0) for i in range(parts)]
    while len(sums) > 1:
        sums = [p + q for p, q in zip(sums[::2], sums[1::2])]
    return jnp.sum(sums[0], axis=0, keepdims=True) * (1.0 / x.shape[0])


def normed(x, gain, bias):
    cen = x - row_mean(x)
    lanes = x.shape[1]
    return (cen * lax.rsqrt(row_mean(cen * cen) + LN_EPS) * widen(gain, lanes) + widen(bias, lanes)).astype(BF16)


def gelu_of_half(h):
    c = 0.7978845608028654
    return h + h * jnp.tanh(h * (2 * c + (8 * c * 0.044715) * (h * h)))


ANY = pl.BlockSpec(memory_space=pl.ANY)


def attn_kernel(x0, x1, x2, x3, w_hbm, b_hbm, g_ref, c_ref, o_ref, y1, qt, kn, vt, sa, sb, w_ref, b_ref, sems):
    bands = (x0, x1, x2, x3)
    first = pl.program_id(0) == 0
    loads = [pltpu.make_async_copy(b_hbm, b_ref, sems.at[3])]
    for t in range(3):
        rows = pl.ds(t * 1152, 1152)
        loads.append(pltpu.make_async_copy(w_hbm.at[rows, :], w_ref.at[rows, :], sems.at[t]))

    @pl.when(first)
    def _():
        loads[0].start()
        loads[1].start()

    for k in range(4):
        y1[:, k * 256:k * 256 + 256] = normed(bands[k][0].astype(F32), g_ref[...], c_ref[...])
    zero8 = jnp.zeros((8, 1024), F32)
    for t in range(3):
        @pl.when(first)
        def _(t=t):
            if t == 0:
                loads[0].wait()
            loads[t + 1].wait()
            if t < 2:
                loads[t + 2].start()

        def proj(i, _, t=t):
            ms = pl.multiple_of(t * 1152 + i * 576, 576)
            acc = dot(w_ref[pl.ds(ms, 576), :], y1[...]) + widen(b_ref[pl.ds(ms, 576), :], 1024)
            for j in range(8):
                part = jnp.concatenate([acc[j * 72:j * 72 + 72], zero8], axis=0)
                if t == 0:
                    qt[i * 8 + j] = part.astype(BF16)
                elif t == 1:
                    kn[i * 8 + j] = part.T.astype(BF16)
                else:
                    vt[i * 8 + j] = part.astype(BF16)
            return 0

        lax.fori_loop(0, 2, proj, 0)
    scale = 1.4426950408889634 * 72 ** -0.5

    def fold(x, op):
        return op(x.reshape(x.shape[0] // 8, 8, x.shape[1]), axis=0)

    def step(ahead, ahead_buf, h, buf, m):
        top, total, acc = None, None, None
        for c in range(4):
            rows = slice(c * 256, c * 256 + 256)
            s = dot(kn[ahead, rows, :], qt[ahead])
            e = jnp.exp2((buf[rows, :] - m) * scale)
            ahead_buf[rows, :] = s
            t, l, o = fold(s, jnp.max), fold(e, jnp.sum), dot(vt[h, :, rows], e.astype(BF16))
            top = t if top is None else jnp.maximum(top, t)
            total = l if total is None else total + l
            acc = o if acc is None else acc + o
        return jnp.max(top, axis=0, keepdims=True), acc[:72] * (1.0 / jnp.sum(total, axis=0, keepdims=True))

    def tiles(i, m):
        m1, one = step(i * 2 + 1, sb, i * 2, sa, m)
        m2, two = step(jnp.minimum(i * 2 + 2, 15), sa, i * 2 + 1, sb, m1)
        o_ref[0, pl.ds(pl.multiple_of(i * 144, 144), 144), :] = jnp.concatenate([one, two], axis=0).astype(BF16)
        return m2

    s0 = dot(kn[0], qt[0])
    sa[...] = s0
    lax.fori_loop(0, 8, tiles, jnp.max(s0, axis=0, keepdims=True))


def whole1(a):
    return pl.BlockSpec(a.shape, lambda i: (0,) * a.ndim, pipeline_mode=pl.Buffered(1))


def attention(xs, at, n, w, b, g, c):
    d = xs[0].shape[1]
    band = pl.BlockSpec((1, d, 256), lambda i: (i + at, 0, 0))
    return pl.pallas_call(
        attn_kernel, grid=(n,),
        in_specs=[band] * 4 + [ANY, ANY, whole1(g), whole1(c)],
        out_specs=pl.BlockSpec((1, d, 1024), lambda i: (i, 0, 0)),
        out_shape=jax.ShapeDtypeStruct((n, d, 1024), BF16),
        scratch_shapes=[pltpu.VMEM((d, 1024), BF16), pltpu.VMEM((16, 80, 1024), BF16), pltpu.VMEM((16, 1024, 80), BF16), pltpu.VMEM((16, 80, 1024), BF16),
                        pltpu.VMEM((1024, 1024), F32), pltpu.VMEM((1024, 1024), F32),
                        pltpu.VMEM(w.shape, BF16), pltpu.VMEM(b.shape, F32), pltpu.SemaphoreType.DMA((4,))],
        name="attn",
        cost_estimate=pl.CostEstimate(flops=n * 25 * 10 ** 9, bytes_accessed=n * 5 * MIB + 10 * MIB, transcendentals=0),
        compiler_params=pltpu.CompilerParams(vmem_limit_bytes=60 * MIB),
    )(*xs, w, b, g, c)


def place_moves(idx, parts, slots, out, buf, sems):
    moves = []
    at = 0
    for ref, (k, start) in zip(parts, slots):
        m = ref.shape[0]
        here = buf.at[pl.ds(at, m)]
        moves.append((pltpu.make_async_copy(ref, here, sems.at[0, len(moves)]),
                      pltpu.make_async_copy(here, out.at[pl.ds(idx[k] + start, m)], sems.at[1, len(moves)])))
        at += m
    return moves


def mlp_kernel(*refs, nb, slots):
    a_ref, bands = refs[0], refs[1:1 + nb]
    wo_hbm, bo, g_ref, c_ref, w1_hbm, b1_hbm, w2_hbm, b2 = refs[1 + nb:9 + nb]
    refs = refs[9 + nb:]
    moves = []
    if slots:
        idx, parts, out, buf, move_sems = refs[0], refs[1:1 + len(slots)], refs[1 + len(slots) + nb], refs[-2], refs[-1]
        moves = place_moves(idx, parts, slots, out, buf, move_sems)
        refs = refs[1 + len(slots):1 + len(slots) + nb] + refs[2 + len(slots) + nb:-2]
    outs = refs[:nb]
    r, y2, hh, wo, w1, b1, w2, sems = refs[nb:]
    lanes = nb * 256
    first = pl.program_id(0) == 0
    ff = w1_hbm.shape[0]
    full = w1.shape[0]
    tile = full // 4
    ups = []
    for j in range(4):
        rows = pl.ds(j * tile, min(tile, ff - j * tile))
        ups.append(pltpu.make_async_copy(w1_hbm.at[rows, :], w1.at[rows, :], sems.at[j]))
    load_o = pltpu.make_async_copy(wo_hbm, wo, sems.at[4])
    load_b = pltpu.make_async_copy(b1_hbm, b1, sems.at[5])
    load_2 = pltpu.make_async_copy(w2_hbm, w2, sems.at[6])

    @pl.when(first)
    def _():
        load_o.start()
        w1[ff:full, :] = jnp.zeros((full - ff, w1.shape[1]), BF16)
        load_o.wait()
        load_b.start()
        ups[0].start()
        ups[1].start()

    for pull, _ in moves:
        pull.start()

    def proj(i, _):
        ms = pl.multiple_of(i * 576, 576)
        t = dot(wo[pl.ds(ms, 576), :], a_ref[0]) + widen(bo[pl.ds(ms, 576), :], lanes)
        for k in range(nb):
            r[pl.ds(ms, 576), k * 256:(k + 1) * 256] = t[:, k * 256:(k + 1) * 256] + bands[k][0, pl.ds(ms, 576), :].astype(F32)
        return 0

    lax.fori_loop(0, 2, proj, 0)

    def norm(i, _):
        ls = pl.multiple_of(i * 256, 256)
        y2[:, pl.ds(ls, 256)] = normed(r[:, pl.ds(ls, 256)], g_ref[...], c_ref[...])
        return 0

    lax.fori_loop(0, nb, norm, 0)

    @pl.when(first)
    def _():
        load_b.wait()

    def up(i, _):
        for j in range(4):
            @pl.when(first & (i == j))
            def _(j=j):
                ups[j].wait()
                if j < 2:
                    ups[j + 2].start()
                elif j == 2:
                    load_2.start()
        ms = pl.multiple_of(i * tile, tile)
        z = dot(w1[pl.ds(ms, tile), :], y2[...]) + widen(b1[pl.ds(ms, tile), :], lanes)
        hh[pl.ds(ms, tile), :] = gelu_of_half(z).astype(BF16)
        return 0

    lax.fori_loop(0, 4, up, 0)
    for pull, push in moves:
        pull.wait()
        push.start()

    @pl.when(first)
    def _():
        load_2.wait()

    def down(i, _):
        ls = pl.multiple_of(i * DOWN, DOWN)
        t = dot(w2[...], hh[:, pl.ds(ls, DOWN)]) + widen(b2[...], DOWN) + r[:, pl.ds(ls, DOWN)]
        t = t.astype(BF16).T
        step = DOWN // 256
        for j in range(nb // step):
            @pl.when(i == j)
            def _():
                for q in range(step):
                    outs[j * step + q][0] = t[q * 256:(q + 1) * 256]
        return 0

    lax.fori_loop(0, lanes // DOWN, down, 0)
    for _, push in moves:
        push.wait()


def mlp(att, xs, at, ks, wo, bo, g, c, w1, b1, w2, b2, idx=None, parts=(), slots=(), shape=None):
    n, d, _ = att.shape
    f = w2.shape[1]
    nb = len(ks)
    lanes = nb * 256
    half = ks[0] // nb
    band = pl.BlockSpec((1, d, 256), lambda i: (i + at, 0, 0))
    extra = [idx, *parts] if parts else []
    total = sum(p.shape[0] for p in parts)
    room = [pltpu.VMEM((total, 256, d), BF16), pltpu.SemaphoreType.DMA((2, len(parts)))] if parts else []
    return pl.pallas_call(
        functools.partial(mlp_kernel, nb=nb, slots=slots), grid=(n,),
        in_specs=[pl.BlockSpec((1, d, lanes), lambda i: (i, 0, half))] + [band] * nb + [ANY, whole1(bo), whole1(g), whole1(c), ANY, ANY, ANY, whole1(b2)]
        + ([pl.BlockSpec(memory_space=pltpu.SMEM)] + [ANY] * len(parts) if parts else []),
        out_specs=[pl.BlockSpec((1, 256, d), lambda i: (i, 0, 0))] * nb + ([ANY] if parts else []),
        out_shape=[jax.ShapeDtypeStruct((n, 256, d), BF16)] * nb + ([shape] if parts else []),
        scratch_shapes=[pltpu.VMEM((d, lanes), F32), pltpu.VMEM((d, lanes), BF16), pltpu.VMEM((f, lanes), BF16),
                        pltpu.VMEM((d, d), BF16), pltpu.VMEM((f, d), BF16), pltpu.VMEM((f, 128), F32), pltpu.VMEM((d, f), BF16),
                        pltpu.SemaphoreType.DMA((7,))] + room,
        name="mlp",
        cost_estimate=pl.CostEstimate(flops=n * nb * 6 * 10 ** 9, bytes_accessed=n * 8 * MIB + 23 * MIB, transcendentals=0),
        compiler_params=pltpu.CompilerParams(vmem_limit_bytes=63 * MIB),
    )(att, *[xs[k] for k in ks], wo, bo, g, c, w1, b1, w2, b2, *extra)


def flip_kernel(w_ref, o_ref, *, rows):
    at = pl.program_id(0) * w_ref.shape[0] + lax.broadcasted_iota(jnp.int32, w_ref.shape, 0)
    o_ref[...] = jnp.where(at < rows, w_ref[...], jnp.zeros_like(w_ref)).T


def flip(w, full, block):
    rows, d = w.shape
    return pl.pallas_call(
        functools.partial(flip_kernel, rows=rows), grid=(full // block,),
        in_specs=[pl.BlockSpec((block, d), lambda i: (i, 0))],
        out_specs=pl.BlockSpec((d, block), lambda i: (0, i)),
        out_shape=jax.ShapeDtypeStruct((d, full), BF16), name="flip",
        cost_estimate=pl.CostEstimate(flops=2 * 10 ** 9, bytes_accessed=20 * MIB, transcendentals=0),
    )(w)


def place_kernel(*refs, slots):
    n = len(slots)
    moves = place_moves(refs[0], refs[1:1 + n], slots, refs[-3], refs[-2], refs[-1])
    for pull, _ in moves:
        pull.start()
    for pull, push in moves:
        pull.wait()
        push.start()
    for _, push in moves:
        push.wait()


def place(idx, parts, slots, out_shape, base=None):
    n = len(parts)
    total = sum(p.shape[0] for p in parts)
    return pl.pallas_call(
        functools.partial(place_kernel, slots=slots),
        in_specs=[pl.BlockSpec(memory_space=pltpu.SMEM)] + [ANY] * (n + (base is not None)),
        out_specs=ANY, out_shape=out_shape, name="place",
        scratch_shapes=[pltpu.VMEM((total,) + parts[0].shape[1:], BF16), pltpu.SemaphoreType.DMA((2, n))],
        input_output_aliases={n + 1: 0} if base is not None else {},
        cost_estimate=pl.CostEstimate(flops=10 ** 9, bytes_accessed=2 * total * 589824, transcendentals=0),
        compiler_params=pltpu.CompilerParams(vmem_limit_bytes=40 * MIB),
    )(idx, *parts, *([base] if base is not None else []))


def column(v, pad=0):
    v = jnp.pad(v, (0, pad)) if pad else v
    return jnp.broadcast_to(v[:, None], (v.shape[0], 128))


def solution(mesh):
    sp = mesh.shape['sp']

    def device_step(images, w_patch, b_patch, pos_embed, ln1_gain, ln1_bias, w_qkv, b_qkv, w_out, b_out, ln2_gain, ln2_bias, w_fc1, b_fc1, w_fc2, b_fc2):
        me = lax.axis_index('sp')
        d = w_patch.shape[3]
        per = images.shape[0] // sp
        planes = jnp.transpose(images, (0, 3, 1, 2))
        x = jnp.arange(512)[:, None]
        o = jnp.arange(512)[None, :]
        px, gx = x % 16, x // 16
        perm = jnp.stack([(o == 128 * (px // 4) + 32 * ((px % 4 + j) % 4) + gx) for j in range(4)]).astype(BF16)
        wp = jnp.transpose(w_patch, (3, 1, 2, 0)).reshape(d, 768)
        pos = pos_embed.T
        bp = column(b_patch)
        wq = jnp.transpose(w_qkv, (1, 2, 3, 0)).reshape(3 * d, d)
        bq = column(b_qkv.reshape(3 * d))
        g1, c1 = column(ln1_gain), column(ln1_bias)
        wo = w_out.reshape(d, d).T
        bo, g2, c2 = column(b_out), column(ln2_gain * 0.5), column(ln2_bias * 0.5)
        pad = 4352 - w_fc1.shape[1]
        w1 = w_fc1.T
        b1 = column(b_fc1 * 0.5, pad)
        w2 = flip(w_fc2, 4352, 256)
        b2 = column(b_fc2)

        def swap(a, k):
            return lax.ppermute(a, 'sp', [(i, i ^ k) for i in range(sp)]) if k else a

        peers = [me ^ k for k in range(sp)]
        starts = [sum(CHUNKS[:c]) for c in range(len(CHUNKS))]
        got, where = [], []
        for c, n in enumerate(GROUPS):
            begin = sum(GROUPS[:c])
            idx = jnp.stack([p * per + begin for p in peers]).astype(jnp.int32)
            mine = embed(idx, planes, perm, wp, bp, pos, n)
            got.append([swap(a, k) for k, a in enumerate(mine)])
            where += [(c, i) for i in range(n)]
        owner = jnp.stack([p * per for p in peers]).astype(jnp.int32)
        early, slots, res = [], [], None
        shape = jax.ShapeDtypeStruct((images.shape[0], 256, d), BF16)
        last = len(CHUNKS) - 1
        for c, n in enumerate(CHUNKS):
            group, at = where[starts[c]]
            xs = got[group]
            if c:
                own, _ = lax.optimization_barrier((xs[0], res[0]))
                xs = [own] + xs[1:]
            att = attention(xs, at, n, wq, bq, g1, c1)
            if c < last:
                res = mlp(att, xs, at, (0, 1, 2, 3), wo, bo, g2, c2, w1, b1, w2, b2)
                back = [swap(a, k) for k, a in enumerate(res)]
                early += back
                slots += [(k, starts[c]) for k in range(sp)]
            else:
                far = mlp(att, xs, at, (2, 3), wo, bo, g2, c2, w1, b1, w2, b2)
                own, _ = lax.optimization_barrier((xs[0], far[0]))
                near = mlp(att, [own] + xs[1:], at, (0, 1), wo, bo, g2, c2, w1, b1, w2, b2, owner, early, slots, shape)
                back = [near[0], swap(near[1], 1), swap(far[0], 2), swap(far[1], 3)]
        return place(owner, back, [(k, starts[last]) for k in range(sp)], shape, near[2])

    in_specs = (P('dp', 'sp', None, None), P(), P(), P('sp', None)) + (P(),) * 12
    return jax.shard_map(device_step, mesh=mesh, in_specs=in_specs, out_specs=P('dp', 'sp', None), check_vma=False)
```

profile of v0, /device:TPU:0, one launch (start us, length us, event | category | flops | bytes accessed | tf_op | source)
XLA Modules:
  0.0 729.6 jit_solution(11263289180566620173)
XLA Ops:
  0.1 2.1 copy.22
  4.0 2.3 copy.23.wp_ref
  10.4 13.7 %embed.3 = (bf16[2,1152,256]{2,1,0:T(8,128)(2,1)}, bf16[2,1152,256]{2,1,0:T(8,128)(2,1)}, bf16[2,1152,256]{2,1,0:T(8,128)(2,1)}, bf16[2,1152,256]{2,1,0:T(8,128)(2,1)}) custom-call(s32[4]{0:T(128)} %pad_add_fusion.idx_ref.refs_11_.refs_0_, f32[32,3,128,512]{3,2,1,0:T(8,128)} %bitcast.19, f32[32,3,128,512]{3,2,1,0:T(8,128)} %bitcast.20, ...), custom_call_target="tpu_custom_call" | custom-call | flops 3623878656 | bytes 12582912 | tf_op jit(solution)/shard_map/embed/pallas_call | solution.py:75
  24.9 2.5 collective-permute-start.1
  28.2 30.1 %embed.2 = (bf16[6,1152,256]{2,1,0:T(8,128)(2,1)}, bf16[6,1152,256]{2,1,0:T(8,128)(2,1)}, bf16[6,1152,256]{2,1,0:T(8,128)(2,1)}, bf16[6,1152,256]{2,1,0:T(8,128)(2,1)}) custom-call(s32[4]{0:T(128)} %pad_add_fusion.1.idx_ref, f32[32,3,128,512]{3,2,1,0:T(8,128)} %bitcast.23, f32[32,3,128,512]{3,2,1,0:T(8,128)} %bitcast.24, f32[32,3,128,512]{3,2,1,0:T(8,128)} %bitcast.25, ...), custom_call_target="tpu_custom_call" | custom-call | flops 10871635968 | bytes 37748736 | tf_op jit(solution)/shard_map/embed/pallas_call | solution.py:75
  58.4 1.9 collective-permute-start.4
  60.5 3.3 copy.25
  63.8 14.7 %flip.1.refs_11_.refs_9_ = bf16[1152,4352]{1,0:T(8,128)(2,1)} custom-call(bf16[4304,1152]{1,0:T(8,128)(2,1)} %w_ref.1), custom_call_target="tpu_custom_call" | custom-call | flops 2000000000 | bytes 20971520 | tf_op jit(solution)/shard_map/flip/pallas_call | solution.py:340
  83.2 67.0 %attn.4.refs_0_ = bf16[2,1152,1024]{2,1,0:T(8,128)(2,1)} custom-call(bf16[2,1152,256]{2,1,0:T(8,128)(2,1)} %get-tuple-element.35.x0.refs_1_, bf16[2,1152,256]{2,1,0:T(8,128)(2,1)} %collective-permute-done.x1.refs_2_, bf16[2,1152,256]{2,1,0:T(8,128)(2,1)} %collective-permute-done.1.x2.refs_3_, bf16[2,1152,256]{2,1,0:T(8,128)(2,1)} %collective-permute-done.2.x3.refs_4_, ...), custom_call_target="tpu_custom_call" | custom-call | flops 49999998976 | bytes 20971520 | tf_op jit(solution)/shard_map/attn/pallas_call | solution.py:186
  154.5 2.0 broadcast_in_dim.28.refs_10_.refs_8_
  156.4 68.8 %mlp.5 = (bf16[2,256,1152]{2,1,0:T(8,128)(2,1)}, bf16[2,256,1152]{2,1,0:T(8,128)(2,1)}, bf16[2,256,1152]{2,1,0:T(8,128)(2,1)}, bf16[2,256,1152]{2,1,0:T(8,128)(2,1)}) custom-call(bf16[2,1152,1024]{2,1,0:T(8,128)(2,1)} %attn.4.refs_0_, bf16[2,1152,256]{2,1,0:T(8,128)(2,1)} %get-tuple-element.35.x0.refs_1_, ...), custom_call_target="tpu_custom_call" | custom-call | flops 48000000000 | bytes 40894464 | tf_op jit(solution)/shard_map/mlp/pallas_call | solution.py:318
  225.6 2.0 collective-permute-start.7
  227.6 3.5 collective-permute-done.5.x3.refs_4_.refs_2_
  231.1 98.0 %attn.5.refs_0_ = bf16[3,1152,1024]{2,1,0:T(8,128)(2,1)} custom-call(bf16[6,1152,256]{2,1,0:T(8,128)(2,1)} %get-tuple-element.49.x0.refs_1_, bf16[6,1152,256]{2,1,0:T(8,128)(2,1)} %collective-permute-done.3.x1.refs_2_, bf16[6,1152,256]{2,1,0:T(8,128)(2,1)} %collective-permute-done.4.x2.refs_3_.refs_1_, ...), custom_call_target="tpu_custom_call" | custom-call | flops 74999996416 | bytes 26214400 | tf_op jit(solution)/shard_map/attn/pallas_call | solution.py:186
  329.1 99.9 %mlp.6 = (bf16[3,256,1152]{2,1,0:T(8,128)(2,1)}, bf16[3,256,1152]{2,1,0:T(8,128)(2,1)}, bf16[3,256,1152]{2,1,0:T(8,128)(2,1)}, bf16[3,256,1152]{2,1,0:T(8,128)(2,1)}) custom-call(bf16[3,1152,1024]{2,1,0:T(8,128)(2,1)} %attn.5.refs_0_, bf16[6,1152,256]{2,1,0:T(8,128)(2,1)} %get-tuple-element.49.x0.refs_1_, ...), custom_call_target="tpu_custom_call" | custom-call | flops 71999995904 | bytes 49283072 | tf_op jit(solution)/shard_map/mlp/pallas_call | solution.py:318
  429.0 67.1 %attn.6.refs_0_ = bf16[2,1152,1024]{2,1,0:T(8,128)(2,1)} custom-call(bf16[6,1152,256]{2,1,0:T(8,128)(2,1)} %get-tuple-element.49.x0.refs_1_, bf16[6,1152,256]{2,1,0:T(8,128)(2,1)} %collective-permute-done.3.x1.refs_2_, bf16[6,1152,256]{2,1,0:T(8,128)(2,1)} %collective-permute-done.4.x2.refs_3_.refs_1_, ...), custom_call_target="tpu_custom_call" | custom-call | flops 49999998976 | bytes 20971520 | tf_op jit(solution)/shard_map/attn/pallas_call | solution.py:186
  496.1 68.9 %mlp.7 = (bf16[2,256,1152]{2,1,0:T(8,128)(2,1)}, bf16[2,256,1152]{2,1,0:T(8,128)(2,1)}, bf16[2,256,1152]{2,1,0:T(8,128)(2,1)}, bf16[2,256,1152]{2,1,0:T(8,128)(2,1)}) custom-call(bf16[2,1152,1024]{2,1,0:T(8,128)(2,1)} %attn.6.refs_0_, bf16[6,1152,256]{2,1,0:T(8,128)(2,1)} %get-tuple-element.49.x0.refs_1_, ...), custom_call_target="tpu_custom_call" | custom-call | flops 48000000000 | bytes 40894464 | tf_op jit(solution)/shard_map/mlp/pallas_call | solution.py:318
  570.0 35.2 %attn.7.refs_0_ = bf16[1,1152,1024]{2,1,0:T(8,128)(2,1)} custom-call(bf16[6,1152,256]{2,1,0:T(8,128)(2,1)} %get-tuple-element.49.x0.refs_1_, bf16[6,1152,256]{2,1,0:T(8,128)(2,1)} %collective-permute-done.3.x1.refs_2_, bf16[6,1152,256]{2,1,0:T(8,128)(2,1)} %collective-permute-done.4.x2.refs_3_.refs_1_, ...), custom_call_target="tpu_custom_call" | custom-call | flops 24999999488 | bytes 15728640 | tf_op jit(solution)/shard_map/attn/pallas_call | solution.py:186
  605.2 21.3 %mlp.8 = (bf16[1,256,1152]{2,1,0:T(8,128)(2,1)}, bf16[1,256,1152]{2,1,0:T(8,128)(2,1)}) custom-call(bf16[1,1152,1024]{2,1,0:T(8,128)(2,1)} %attn.7.refs_0_, bf16[6,1152,256]{2,1,0:T(8,128)(2,1)} %collective-permute-done.4.x2.refs_3_.refs_1_, bf16[6,1152,256]{2,1,0:T(8,128)(2,1)} %collective-permute-done.5.x3.refs_4_.refs_2_, bf16[1152,1152]{1,0:T(8,128)(2,1)} %bitcast.30, ...), custom_call_target="tpu_custom_call" | custom-call | flops 12000000000 | bytes 32505856 | tf_op jit(solution)/shard_map/mlp/pallas_call | solution.py:318
  626.5 44.0 %collective-permute-done.13.refs_22_ = bf16[2,256,1152]{2,1,0:T(8,128)(2,1)} collective-permute-done((bf16[2,256,1152]{2,1,0:T(8,128)(2,1)}, bf16[2,256,1152]{2,1,0:T(8,128)(2,1)}, u32[]{:S(2)}, u32[]{:S(2)}) %collective-permute-start.13) | collective-permute-done | bytes 1179680 | tf_op jit(solution)/shard_map/ppermute | solution.py:407
  672.2 22.8 %collective-permute-done.14.refs_23_ = bf16[2,256,1152]{2,1,0:T(8,128)(2,1)} collective-permute-done((bf16[2,256,1152]{2,1,0:T(8,128)(2,1)}, bf16[2,256,1152]{2,1,0:T(8,128)(2,1)}, u32[]{:S(2)}, u32[]{:S(2)}) %collective-permute-start.14) | collective-permute-done | bytes 1179680 | tf_op jit(solution)/shard_map/ppermute | solution.py:407
  697.0 25.8 %mlp.9 = (bf16[1,256,1152]{2,1,0:T(8,128)(2,1)}, bf16[1,256,1152]{2,1,0:T(8,128)(2,1)}, bf16[32,256,1152]{2,1,0:T(8,128)(2,1)}) custom-call(bf16[1,1152,1024]{2,1,0:T(8,128)(2,1)} %attn.7.refs_0_, bf16[6,1152,256]{2,1,0:T(8,128)(2,1)} %get-tuple-element.49.x0.refs_1_, bf16[6,1152,256]{2,1,0:T(8,128)(2,1)} %collective-permute-done.3.x1.refs_2_, ...), custom_call_target="tpu_custom_call" | custom-call | flops 12000000000 | bytes 32505856 | tf_op jit(solution)/shard_map/mlp/pallas_call | solution.py:318
  722.8 2.2 collective-permute-done.15.refs_2_
  726.1 3.3 place.1
  (76 shorter events, 26.8 us)
Async XLA Ops:
  24.1 54.5 %collective-permute-start = (bf16[2,1152,256]{2,1,0:T(8,128)(2,1)}, bf16[2,1152,256]{2,1,0:T(8,128)(2,1)}, u32[]{:S(2)}, u32[]{:S(2)}) collective-permute-start(bf16[2,1152,256]{2,1,0:T(8,128)(2,1)} %get-tuple-element.36), channel_id=1, source_target_pairs={{0,1},{1,0},{2,3},{3,2},{4,5},{5,4},{6,7},{7,6}} | collective-permute-start | bytes 3538952 | tf_op jit(solution)/shard_map/ppermute | solution.py:407
  24.9 53.7 %collective-permute-start.1 = (bf16[2,1152,256]{2,1,0:T(8,128)(2,1)}, bf16[2,1152,256]{2,1,0:T(8,128)(2,1)}, u32[]{:S(2)}, u32[]{:S(2)}) collective-permute-start(bf16[2,1152,256]{2,1,0:T(8,128)(2,1)} %get-tuple-element.37), channel_id=1, source_target_pairs={{0,2},{1,3},{2,0},{3,1},{4,6},{5,7},{6,4},{7,5}} | collective-permute-start | bytes 3538952 | tf_op jit(solution)/shard_map/ppermute | solution.py:407
  27.4 52.0 %collective-permute-start.2 = (bf16[2,1152,256]{2,1,0:T(8,128)(2,1)}, bf16[2,1152,256]{2,1,0:T(8,128)(2,1)}, u32[]{:S(2)}, u32[]{:S(2)}) collective-permute-start(bf16[2,1152,256]{2,1,0:T(8,128)(2,1)} %get-tuple-element.38), channel_id=1, source_target_pairs={{0,3},{1,2},{2,1},{3,0},{4,7},{5,6},{6,5},{7,4}} | collective-permute-start | bytes 3538952 | tf_op jit(solution)/shard_map/ppermute | solution.py:407
  28.2 32.2 %copy-start.3 = (f32[3,16,72]{2,1,0:T(8,128)S(1)}, f32[3,16,72]{2,1,0:T(8,128)}, u32[]{:S(2)}) copy-start(f32[3,16,72]{2,1,0:T(8,128)} %param.23) | copy-start | bytes 41476
  28.2 32.3 %copy-start.2 = (bf16[16,72,1152]{2,1,0:T(8,128)(2,1)S(1)}, bf16[16,72,1152]{2,1,0:T(8,128)(2,1)}, u32[]{:S(2)}) copy-start(bf16[16,72,1152]{2,1,0:T(8,128)(2,1)} %param.24) | copy-start | bytes 7962628
  58.3 169.3 %collective-permute-start.3 = (bf16[6,1152,256]{2,1,0:T(8,128)(2,1)}, bf16[6,1152,256]{2,1,0:T(8,128)(2,1)}, u32[]{:S(2)}, u32[]{:S(2)}) collective-permute-start(bf16[6,1152,256]{2,1,0:T(8,128)(2,1)} %get-tuple-element.41), channel_id=1, source_target_pairs={{0,1},{1,0},{2,3},{3,2},{4,5},{5,4},{6,7},{7,6}} | collective-permute-start | bytes 10616840 | tf_op jit(solution)/shard_map/ppermute | solution.py:407
  58.4 169.1 %collective-permute-start.4 = (bf16[6,1152,256]{2,1,0:T(8,128)(2,1)}, bf16[6,1152,256]{2,1,0:T(8,128)(2,1)}, u32[]{:S(2)}, u32[]{:S(2)}) collective-permute-start(bf16[6,1152,256]{2,1,0:T(8,128)(2,1)} %get-tuple-element.42), channel_id=1, source_target_pairs={{0,2},{1,3},{2,0},{3,1},{4,6},{5,7},{6,4},{7,5}} | collective-permute-start | bytes 10616840 | tf_op jit(solution)/shard_map/ppermute | solution.py:407
  63.8 15.6 %copy-start.6 = (f32[1152]{0:T(1024)S(1)}, f32[1152]{0:T(1024)}, u32[]{:S(2)}) copy-start(f32[1152]{0:T(1024)} %param.20) | copy-start | bytes 13828
  63.8 16.6 %copy-start.7 = (f32[1152]{0:T(1024)S(1)}, f32[1152]{0:T(1024)}, u32[]{:S(2)}) copy-start(f32[1152]{0:T(1024)} %param.21) | copy-start | bytes 13828
  78.6 152.5 %collective-permute-start.5 = (bf16[6,1152,256]{2,1,0:T(8,128)(2,1)}, bf16[6,1152,256]{2,1,0:T(8,128)(2,1)}, u32[]{:S(2)}, u32[]{:S(2)}) collective-permute-start(bf16[6,1152,256]{2,1,0:T(8,128)(2,1)} %get-tuple-element.43), channel_id=1, source_target_pairs={{0,3},{1,2},{2,1},{3,0},{4,7},{5,6},{6,5},{7,4}} | collective-permute-start | bytes 10616840 | tf_op jit(solution)/shard_map/ppermute | solution.py:407
  83.2 69.1 %copy-start.8 = (f32[1152]{0:T(1024)S(1)}, f32[1152]{0:T(1024)}, u32[]{:S(2)}) copy-start(f32[1152]{0:T(1024)} %param.25) | copy-start | bytes 13828
  225.3 340.2 %collective-permute-start.6 = (bf16[2,256,1152]{2,1,0:T(8,128)(2,1)}, bf16[2,256,1152]{2,1,0:T(8,128)(2,1)}, u32[]{:S(2)}, u32[]{:S(2)}) collective-permute-start(bf16[2,256,1152]{2,1,0:T(8,128)(2,1)} %get-tuple-element.50), channel_id=1, source_target_pairs={{0,1},{1,0},{2,3},{3,2},{4,5},{5,4},{6,7},{7,6}} | collective-permute-start | bytes 3538952 | tf_op jit(solution)/shard_map/ppermute | solution.py:407
  225.6 341.7 %collective-permute-start.7 = (bf16[2,256,1152]{2,1,0:T(8,128)(2,1)}, bf16[2,256,1152]{2,1,0:T(8,128)(2,1)}, u32[]{:S(2)}, u32[]{:S(2)}) collective-permute-start(bf16[2,256,1152]{2,1,0:T(8,128)(2,1)} %get-tuple-element.51), channel_id=1, source_target_pairs={{0,2},{1,3},{2,0},{3,1},{4,6},{5,7},{6,4},{7,5}} | collective-permute-start | bytes 3538952 | tf_op jit(solution)/shard_map/ppermute | solution.py:407
  227.6 339.8 %collective-permute-start.8 = (bf16[2,256,1152]{2,1,0:T(8,128)(2,1)}, bf16[2,256,1152]{2,1,0:T(8,128)(2,1)}, u32[]{:S(2)}, u32[]{:S(2)}) collective-permute-start(bf16[2,256,1152]{2,1,0:T(8,128)(2,1)} %get-tuple-element.52), channel_id=1, source_target_pairs={{0,3},{1,2},{2,1},{3,0},{4,7},{5,6},{6,5},{7,4}} | collective-permute-start | bytes 3538952 | tf_op jit(solution)/shard_map/ppermute | solution.py:407
  564.9 4.2 collective-permute-start.12
  565.2 131.8 %collective-permute-start.9 = (bf16[3,256,1152]{2,1,0:T(8,128)(2,1)}, bf16[3,256,1152]{2,1,0:T(8,128)(2,1)}, u32[]{:S(2)}, u32[]{:S(2)}) collective-permute-start(bf16[3,256,1152]{2,1,0:T(8,128)(2,1)} %get-tuple-element.53), channel_id=1, source_target_pairs={{0,1},{1,0},{2,3},{3,2},{4,5},{5,4},{6,7},{7,6}} | collective-permute-start | bytes 5308424 | tf_op jit(solution)/shard_map/ppermute | solution.py:407
  565.5 131.5 %collective-permute-start.10 = (bf16[3,256,1152]{2,1,0:T(8,128)(2,1)}, bf16[3,256,1152]{2,1,0:T(8,128)(2,1)}, u32[]{:S(2)}, u32[]{:S(2)}) collective-permute-start(bf16[3,256,1152]{2,1,0:T(8,128)(2,1)} %get-tuple-element.54), channel_id=1, source_target_pairs={{0,2},{1,3},{2,0},{3,1},{4,6},{5,7},{6,4},{7,5}} | collective-permute-start | bytes 5308424 | tf_op jit(solution)/shard_map/ppermute | solution.py:407
  567.3 129.7 %collective-permute-start.11 = (bf16[3,256,1152]{2,1,0:T(8,128)(2,1)}, bf16[3,256,1152]{2,1,0:T(8,128)(2,1)}, u32[]{:S(2)}, u32[]{:S(2)}) collective-permute-start(bf16[3,256,1152]{2,1,0:T(8,128)(2,1)} %get-tuple-element.55), channel_id=1, source_target_pairs={{0,3},{1,2},{2,1},{3,0},{4,7},{5,6},{6,5},{7,4}} | collective-permute-start | bytes 5308424 | tf_op jit(solution)/shard_map/ppermute | solution.py:407
  567.4 103.1 %collective-permute-start.13 = (bf16[2,256,1152]{2,1,0:T(8,128)(2,1)}, bf16[2,256,1152]{2,1,0:T(8,128)(2,1)}, u32[]{:S(2)}, u32[]{:S(2)}) collective-permute-start(bf16[2,256,1152]{2,1,0:T(8,128)(2,1)} %get-tuple-element.57), channel_id=1, source_target_pairs={{0,2},{1,3},{2,0},{3,1},{4,6},{5,7},{6,4},{7,5}} | collective-permute-start | bytes 3538952 | tf_op jit(solution)/shard_map/ppermute | solution.py:407
  569.1 126.0 %collective-permute-start.14 = (bf16[2,256,1152]{2,1,0:T(8,128)(2,1)}, bf16[2,256,1152]{2,1,0:T(8,128)(2,1)}, u32[]{:S(2)}, u32[]{:S(2)}) collective-permute-start(bf16[2,256,1152]{2,1,0:T(8,128)(2,1)} %get-tuple-element.58), channel_id=1, source_target_pairs={{0,3},{1,2},{2,1},{3,0},{4,7},{5,6},{6,5},{7,4}} | collective-permute-start | bytes 3538952 | tf_op jit(solution)/shard_map/ppermute | solution.py:407
  670.5 52.3 %collective-permute-start.16 = (bf16[1,256,1152]{2,1,0:T(8,128)(2,1)}, bf16[1,256,1152]{2,1,0:T(8,128)(2,1)S(1)}, u32[]{:S(2)}, u32[]{:S(2)}) collective-permute-start(bf16[1,256,1152]{2,1,0:T(8,128)(2,1)} %get-tuple-element.48), channel_id=1, source_target_pairs={{0,2},{1,3},{2,0},{3,1},{4,6},{5,7},{6,4},{7,5}} | collective-permute-start | bytes 1769480 | tf_op jit(solution)/shard_map/ppermute | solution.py:407
  695.0 29.9 %copy-start.1 = (s32[4]{0:T(128)S(1)}, s32[4]{0:T(128)}, u32[]{:S(2)}) copy-start(s32[4]{0:T(128)} %pad_add_fusion.idx_ref.refs_11_.refs_0_) | copy-start | bytes 52
  695.0 27.7 %collective-permute-start.17 = (bf16[1,256,1152]{2,1,0:T(8,128)(2,1)}, bf16[1,256,1152]{2,1,0:T(8,128)(2,1)}, u32[]{:S(2)}, u32[]{:S(2)}) collective-permute-start(bf16[1,256,1152]{2,1,0:T(8,128)(2,1)} %get-tuple-element.61), channel_id=1, source_target_pairs={{0,3},{1,2},{2,1},{3,0},{4,7},{5,6},{6,5},{7,4}} | collective-permute-start | bytes 1769480 | tf_op jit(solution)/shard_map/ppermute | solution.py:407
  722.8 2.2 collective-permute-start.15
  (6 other events, 39.8 us)
where the time goes:
time: 736 us; the launch traced here: 730 us
  Pallas kernels  614 us (83%)
  waiting for transfers between devices  73.3 us (10%)
  local copies, waits for them, and re-layouts  21.7 us (3%)
  starting transfers between devices  16.6 us (2%)
    pallas_call x5, Pallas kernels, mlp(): pl.pallas_call(functools.partial(mlp_kernel, nb=nb, slots=slots), grid=(n...  285 us
    pallas_call x4, Pallas kernels, attention(): pl.pallas_call(attn_kernel, grid=(n,), in_specs=[band] * 4 + [ANY, ANY, w...  267 us
    ppermute x18, waiting for transfers between devices, swap(): return lax.ppermute(a, 'sp', [(i, i ^ k) for i in range(sp)]) if k else a  73.3 us
    pallas_call x2, Pallas kernels, embed(): pl.pallas_call(embed_kernel, grid_spec=pltpu.PrefetchScalarGridSpec(num_s...  43.8 us
    ppermute x18, starting transfers between devices, swap(): return lax.ppermute(a, 'sp', [(i, i ^ k) for i in range(sp)]) if k else a  16.6 us
    pallas_call x1, Pallas kernels, flip(): pl.pallas_call(functools.partial(flip_kernel, rows=rows), grid=(full // b...  14.7 us
  transfers between devices with their start and end apart: 18, of which 5 were waited for; matrix products, arithmetic and copies ran while one was open for 2% of the time, Pallas kernels for 82%

commit v1 on v0

--- a/solution.py
+++ b/solution.py
@@ -133,20 +133,20 @@
             if t < 2:
                 loads[t + 2].start()
 
-        def proj(i, _, t=t):
-            ms = pl.multiple_of(t * 1152 + i * 576, 576)
-            acc = dot(w_ref[pl.ds(ms, 576), :], y1[...]) + widen(b_ref[pl.ds(ms, 576), :], 1024)
-            for j in range(8):
+        def proj(t=t):
+            rows = slice(t * 1152, t * 1152 + 1152)
+            acc = dot(w_ref[rows, :], y1[...]) + widen(b_ref[rows, :], 1024)
+            for j in range(16):
                 part = jnp.concatenate([acc[j * 72:j * 72 + 72], zero8], axis=0)
                 if t == 0:
-                    qt[i * 8 + j] = part.astype(BF16)
+                    qt[j] = part.astype(BF16)
                 elif t == 1:
-                    kn[i * 8 + j] = part.T.astype(BF16)
+                    kn[j] = part.T.astype(BF16)
                 else:
-                    vt[i * 8 + j] = part.astype(BF16)
+                    vt[j] = part.astype(BF16)
             return 0
 
-        lax.fori_loop(0, 2, proj, 0)
+        proj()
     scale = 1.4426950408889634 * 72 ** -0.5
 
     def fold(x, op):
@@ -400,7 +400,7 @@
         pad = 4352 - w_fc1.shape[1]
         w1 = w_fc1.T
         b1 = column(b_fc1 * 0.5, pad)
-        w2 = flip(w_fc2, 4352, 256)
+        w2 = flip(w_fc2, 4352, 2176)
         b2 = column(b_fc2)
 
         def swap(a, k):

time: 736 us -> 734 us (level)
  Pallas kernels: 614 us -> 602 us
  waiting for transfers between devices: 73.3 us -> 82.1 us
    ppermute x18, waiting for transfers between devices: 73.3 us -> 82.1 us  [swap(): return lax.ppermute(a, 'sp', [(i, i ^ k) for i in range(sp)]) if k else a]
  transfers between devices with their start and end apart: 18 -> 18, of which waited for: 5 -> 5; matrix products, arithmetic and copies ran while one was open for 2% -> 2% of each run, Pallas kernels for 82% -> 80%
where the time goes in v1:
time: 734 us; the launch traced here: 727 us
  Pallas kernels  602 us (82%)
  waiting for transfers between devices  82.1 us (11%)
  local copies, waits for them, and re-layouts  21.7 us (3%)
  starting transfers between devices  16.6 us (2%)
    pallas_call x5, Pallas kernels, mlp(): pl.pallas_call(functools.partial(mlp_kernel, nb=nb, slots=slots), grid=(n...  285 us
    pallas_call x4, Pallas kernels, attention(): pl.pallas_call(attn_kernel, grid=(n,), in_specs=[band] * 4 + [ANY, ANY, w...  262 us
    ppermute x18, waiting for transfers between devices, swap(): return lax.ppermute(a, 'sp', [(i, i ^ k) for i in range(sp)]) if k else a  82.1 us
    pallas_call x2, Pallas kernels, embed(): pl.pallas_call(embed_kernel, grid_spec=pltpu.PrefetchScalarGridSpec(num_s...  43.8 us
    ppermute x18, starting transfers between devices, swap(): return lax.ppermute(a, 'sp', [(i, i ^ k) for i in range(sp)]) if k else a  16.6 us
  transfers between devices with their start and end apart: 18, of which 5 were waited for; matrix products, arithmetic and copies ran while one was open for 2% of the time, Pallas kernels for 80%

profile of v1, /device:TPU:0, one launch (start us, length us, event | category | flops | bytes accessed | tf_op | source)
XLA Modules:
  0.0 726.6 jit_solution(10179748520868880754)
XLA Ops:
  0.1 2.1 copy.22
  4.0 2.3 copy.23.wp_ref
  10.4 13.7 %embed.3 = (bf16[2,1152,256]{2,1,0:T(8,128)(2,1)}, bf16[2,1152,256]{2,1,0:T(8,128)(2,1)}, bf16[2,1152,256]{2,1,0:T(8,128)(2,1)}, bf16[2,1152,256]{2,1,0:T(8,128)(2,1)}) custom-call(s32[4]{0:T(128)} %pad_add_fusion.idx_ref.refs_11_.refs_0_, f32[32,3,128,512]{3,2,1,0:T(8,128)} %bitcast.19, f32[32,3,128,512]{3,2,1,0:T(8,128)} %bitcast.20, ...), custom_call_target="tpu_custom_call" | custom-call | flops 3623878656 | bytes 12582912 | tf_op jit(solution)/shard_map/embed/pallas_call | solution.py:75
  24.9 2.5 collective-permute-start.1
  28.2 30.1 %embed.2 = (bf16[6,1152,256]{2,1,0:T(8,128)(2,1)}, bf16[6,1152,256]{2,1,0:T(8,128)(2,1)}, bf16[6,1152,256]{2,1,0:T(8,128)(2,1)}, bf16[6,1152,256]{2,1,0:T(8,128)(2,1)}) custom-call(s32[4]{0:T(128)} %pad_add_fusion.1.idx_ref, f32[32,3,128,512]{3,2,1,0:T(8,128)} %bitcast.23, f32[32,3,128,512]{3,2,1,0:T(8,128)} %bitcast.24, f32[32,3,128,512]{3,2,1,0:T(8,128)} %bitcast.25, ...), custom_call_target="tpu_custom_call" | custom-call | flops 10871635968 | bytes 37748736 | tf_op jit(solution)/shard_map/embed/pallas_call | solution.py:75
  60.5 3.3 copy.25
  63.8 7.6 %flip.1.refs_11_.refs_9_ = bf16[1152,4352]{1,0:T(8,128)(2,1)} custom-call(bf16[4304,1152]{1,0:T(8,128)(2,1)} %w_ref.1), custom_call_target="tpu_custom_call" | custom-call | flops 2000000000 | bytes 20971520 | tf_op jit(solution)/shard_map/flip/pallas_call | solution.py:340
  71.5 7.9 %collective-permute-done.2.x3.refs_4_ = bf16[2,1152,256]{2,1,0:T(8,128)(2,1)} collective-permute-done((bf16[2,1152,256]{2,1,0:T(8,128)(2,1)}, bf16[2,1152,256]{2,1,0:T(8,128)(2,1)}, u32[]{:S(2)}, u32[]{:S(2)}) %collective-permute-start.2) | collective-permute-done | bytes 1179680 | tf_op jit(solution)/shard_map/ppermute | solution.py:407
  83.2 65.9 %attn.4.refs_0_ = bf16[2,1152,1024]{2,1,0:T(8,128)(2,1)} custom-call(bf16[2,1152,256]{2,1,0:T(8,128)(2,1)} %get-tuple-element.35.x0.refs_1_, bf16[2,1152,256]{2,1,0:T(8,128)(2,1)} %collective-permute-done.x1.refs_2_, bf16[2,1152,256]{2,1,0:T(8,128)(2,1)} %collective-permute-done.1.x2.refs_3_, bf16[2,1152,256]{2,1,0:T(8,128)(2,1)} %collective-permute-done.2.x3.refs_4_, ...), custom_call_target="tpu_custom_call" | custom-call | flops 49999998976 | bytes 20971520 | tf_op jit(solution)/shard_map/attn/pallas_call | solution.py:186
  153.3 2.0 broadcast_in_dim.28.refs_10_.refs_8_
  155.3 68.7 %mlp.5 = (bf16[2,256,1152]{2,1,0:T(8,128)(2,1)}, bf16[2,256,1152]{2,1,0:T(8,128)(2,1)}, bf16[2,256,1152]{2,1,0:T(8,128)(2,1)}, bf16[2,256,1152]{2,1,0:T(8,128)(2,1)}) custom-call(bf16[2,1152,1024]{2,1,0:T(8,128)(2,1)} %attn.4.refs_0_, bf16[2,1152,256]{2,1,0:T(8,128)(2,1)} %get-tuple-element.35.x0.refs_1_, ...), custom_call_target="tpu_custom_call" | custom-call | flops 48000000000 | bytes 40894464 | tf_op jit(solution)/shard_map/mlp/pallas_call | solution.py:318
  224.3 2.0 collective-permute-start.7
  226.3 4.8 collective-permute-done.5.x3.refs_4_.refs_2_
  231.1 96.1 %attn.5.refs_0_ = bf16[3,1152,1024]{2,1,0:T(8,128)(2,1)} custom-call(bf16[6,1152,256]{2,1,0:T(8,128)(2,1)} %get-tuple-element.49.x0.refs_1_, bf16[6,1152,256]{2,1,0:T(8,128)(2,1)} %collective-permute-done.3.x1.refs_2_, bf16[6,1152,256]{2,1,0:T(8,128)(2,1)} %collective-permute-done.4.x2.refs_3_.refs_1_, ...), custom_call_target="tpu_custom_call" | custom-call | flops 74999996416 | bytes 26214400 | tf_op jit(solution)/shard_map/attn/pallas_call | solution.py:186
  327.2 99.8 %mlp.6 = (bf16[3,256,1152]{2,1,0:T(8,128)(2,1)}, bf16[3,256,1152]{2,1,0:T(8,128)(2,1)}, bf16[3,256,1152]{2,1,0:T(8,128)(2,1)}, bf16[3,256,1152]{2,1,0:T(8,128)(2,1)}) custom-call(bf16[3,1152,1024]{2,1,0:T(8,128)(2,1)} %attn.5.refs_0_, bf16[6,1152,256]{2,1,0:T(8,128)(2,1)} %get-tuple-element.49.x0.refs_1_, ...), custom_call_target="tpu_custom_call" | custom-call | flops 71999995904 | bytes 49283072 | tf_op jit(solution)/shard_map/mlp/pallas_call | solution.py:318
  427.0 65.8 %attn.6.refs_0_ = bf16[2,1152,1024]{2,1,0:T(8,128)(2,1)} custom-call(bf16[6,1152,256]{2,1,0:T(8,128)(2,1)} %get-tuple-element.49.x0.refs_1_, bf16[6,1152,256]{2,1,0:T(8,128)(2,1)} %collective-permute-done.3.x1.refs_2_, bf16[6,1152,256]{2,1,0:T(8,128)(2,1)} %collective-permute-done.4.x2.refs_3_.refs_1_, ...), custom_call_target="tpu_custom_call" | custom-call | flops 49999998976 | bytes 20971520 | tf_op jit(solution)/shard_map/attn/pallas_call | solution.py:186
  492.9 69.1 %mlp.7 = (bf16[2,256,1152]{2,1,0:T(8,128)(2,1)}, bf16[2,256,1152]{2,1,0:T(8,128)(2,1)}, bf16[2,256,1152]{2,1,0:T(8,128)(2,1)}, bf16[2,256,1152]{2,1,0:T(8,128)(2,1)}) custom-call(bf16[2,1152,1024]{2,1,0:T(8,128)(2,1)} %attn.6.refs_0_, bf16[6,1152,256]{2,1,0:T(8,128)(2,1)} %get-tuple-element.49.x0.refs_1_, ...), custom_call_target="tpu_custom_call" | custom-call | flops 48000000000 | bytes 40894464 | tf_op jit(solution)/shard_map/mlp/pallas_call | solution.py:318
  567.1 34.6 %attn.7.refs_0_ = bf16[1,1152,1024]{2,1,0:T(8,128)(2,1)} custom-call(bf16[6,1152,256]{2,1,0:T(8,128)(2,1)} %get-tuple-element.49.x0.refs_1_, bf16[6,1152,256]{2,1,0:T(8,128)(2,1)} %collective-permute-done.3.x1.refs_2_, bf16[6,1152,256]{2,1,0:T(8,128)(2,1)} %collective-permute-done.4.x2.refs_3_.refs_1_, ...), custom_call_target="tpu_custom_call" | custom-call | flops 24999999488 | bytes 15728640 | tf_op jit(solution)/shard_map/attn/pallas_call | solution.py:186
  601.6 21.5 %mlp.8 = (bf16[1,256,1152]{2,1,0:T(8,128)(2,1)}, bf16[1,256,1152]{2,1,0:T(8,128)(2,1)}) custom-call(bf16[1,1152,1024]{2,1,0:T(8,128)(2,1)} %attn.7.refs_0_, bf16[6,1152,256]{2,1,0:T(8,128)(2,1)} %collective-permute-done.4.x2.refs_3_.refs_1_, bf16[6,1152,256]{2,1,0:T(8,128)(2,1)} %collective-permute-done.5.x3.refs_4_.refs_2_, bf16[1152,1152]{1,0:T(8,128)(2,1)} %bitcast.30, ...), custom_call_target="tpu_custom_call" | custom-call | flops 12000000000 | bytes 32505856 | tf_op jit(solution)/shard_map/mlp/pallas_call | solution.py:318
  623.1 44.4 %collective-permute-done.13.refs_22_ = bf16[2,256,1152]{2,1,0:T(8,128)(2,1)} collective-permute-done((bf16[2,256,1152]{2,1,0:T(8,128)(2,1)}, bf16[2,256,1152]{2,1,0:T(8,128)(2,1)}, u32[]{:S(2)}, u32[]{:S(2)}) %collective-permute-start.13) | collective-permute-done | bytes 1179680 | tf_op jit(solution)/shard_map/ppermute | solution.py:407
  669.3 22.8 %collective-permute-done.14.refs_23_ = bf16[2,256,1152]{2,1,0:T(8,128)(2,1)} collective-permute-done((bf16[2,256,1152]{2,1,0:T(8,128)(2,1)}, bf16[2,256,1152]{2,1,0:T(8,128)(2,1)}, u32[]{:S(2)}, u32[]{:S(2)}) %collective-permute-start.14) | collective-permute-done | bytes 1179680 | tf_op jit(solution)/shard_map/ppermute | solution.py:407
  694.0 25.5 %mlp.9 = (bf16[1,256,1152]{2,1,0:T(8,128)(2,1)}, bf16[1,256,1152]{2,1,0:T(8,128)(2,1)}, bf16[32,256,1152]{2,1,0:T(8,128)(2,1)}) custom-call(bf16[1,1152,1024]{2,1,0:T(8,128)(2,1)} %attn.7.refs_0_, bf16[6,1152,256]{2,1,0:T(8,128)(2,1)} %get-tuple-element.49.x0.refs_1_, bf16[6,1152,256]{2,1,0:T(8,128)(2,1)} %collective-permute-done.3.x1.refs_2_, ...), custom_call_target="tpu_custom_call" | custom-call | flops 12000000000 | bytes 32505856 | tf_op jit(solution)/shard_map/mlp/pallas_call | solution.py:318
  719.6 2.2 collective-permute-done.15.refs_2_
  722.9 3.3 place.1
  (76 shorter events, 28.0 us)
Async XLA Ops:
  24.1 47.4 %collective-permute-start = (bf16[2,1152,256]{2,1,0:T(8,128)(2,1)}, bf16[2,1152,256]{2,1,0:T(8,128)(2,1)}, u32[]{:S(2)}, u32[]{:S(2)}) collective-permute-start(bf16[2,1152,256]{2,1,0:T(8,128)(2,1)} %get-tuple-element.36), channel_id=1, source_target_pairs={{0,1},{1,0},{2,3},{3,2},{4,5},{5,4},{6,7},{7,6}} | collective-permute-start | bytes 3538952 | tf_op jit(solution)/shard_map/ppermute | solution.py:407
  24.9 46.6 %collective-permute-start.1 = (bf16[2,1152,256]{2,1,0:T(8,128)(2,1)}, bf16[2,1152,256]{2,1,0:T(8,128)(2,1)}, u32[]{:S(2)}, u32[]{:S(2)}) collective-permute-start(bf16[2,1152,256]{2,1,0:T(8,128)(2,1)} %get-tuple-element.37), channel_id=1, source_target_pairs={{0,2},{1,3},{2,0},{3,1},{4,6},{5,7},{6,4},{7,5}} | collective-permute-start | bytes 3538952 | tf_op jit(solution)/shard_map/ppermute | solution.py:407
  27.4 52.0 %collective-permute-start.2 = (bf16[2,1152,256]{2,1,0:T(8,128)(2,1)}, bf16[2,1152,256]{2,1,0:T(8,128)(2,1)}, u32[]{:S(2)}, u32[]{:S(2)}) collective-permute-start(bf16[2,1152,256]{2,1,0:T(8,128)(2,1)} %get-tuple-element.38), channel_id=1, source_target_pairs={{0,3},{1,2},{2,1},{3,0},{4,7},{5,6},{6,5},{7,4}} | collective-permute-start | bytes 3538952 | tf_op jit(solution)/shard_map/ppermute | solution.py:407
  28.2 32.2 %copy-start.3 = (f32[3,16,72]{2,1,0:T(8,128)S(1)}, f32[3,16,72]{2,1,0:T(8,128)}, u32[]{:S(2)}) copy-start(f32[3,16,72]{2,1,0:T(8,128)} %param.23) | copy-start | bytes 41476
  28.2 32.3 %copy-start.2 = (bf16[16,72,1152]{2,1,0:T(8,128)(2,1)S(1)}, bf16[16,72,1152]{2,1,0:T(8,128)(2,1)}, u32[]{:S(2)}) copy-start(bf16[16,72,1152]{2,1,0:T(8,128)(2,1)} %param.24) | copy-start | bytes 7962628
  58.3 167.9 %collective-permute-start.3 = (bf16[6,1152,256]{2,1,0:T(8,128)(2,1)}, bf16[6,1152,256]{2,1,0:T(8,128)(2,1)}, u32[]{:S(2)}, u32[]{:S(2)}) collective-permute-start(bf16[6,1152,256]{2,1,0:T(8,128)(2,1)} %get-tuple-element.41), channel_id=1, source_target_pairs={{0,1},{1,0},{2,3},{3,2},{4,5},{5,4},{6,7},{7,6}} | collective-permute-start | bytes 10616840 | tf_op jit(solution)/shard_map/ppermute | solution.py:407
  58.4 167.8 %collective-permute-start.4 = (bf16[6,1152,256]{2,1,0:T(8,128)(2,1)}, bf16[6,1152,256]{2,1,0:T(8,128)(2,1)}, u32[]{:S(2)}, u32[]{:S(2)}) collective-permute-start(bf16[6,1152,256]{2,1,0:T(8,128)(2,1)} %get-tuple-element.42), channel_id=1, source_target_pairs={{0,2},{1,3},{2,0},{3,1},{4,6},{5,7},{6,4},{7,5}} | collective-permute-start | bytes 10616840 | tf_op jit(solution)/shard_map/ppermute | solution.py:407
  63.8 15.6 %copy-start.6 = (f32[1152]{0:T(1024)S(1)}, f32[1152]{0:T(1024)}, u32[]{:S(2)}) copy-start(f32[1152]{0:T(1024)} %param.20) | copy-start | bytes 13828
  63.8 16.6 %copy-start.7 = (f32[1152]{0:T(1024)S(1)}, f32[1152]{0:T(1024)}, u32[]{:S(2)}) copy-start(f32[1152]{0:T(1024)} %param.21) | copy-start | bytes 13828
  71.5 159.6 %collective-permute-start.5 = (bf16[6,1152,256]{2,1,0:T(8,128)(2,1)}, bf16[6,1152,256]{2,1,0:T(8,128)(2,1)}, u32[]{:S(2)}, u32[]{:S(2)}) collective-permute-start(bf16[6,1152,256]{2,1,0:T(8,128)(2,1)} %get-tuple-element.43), channel_id=1, source_target_pairs={{0,3},{1,2},{2,1},{3,0},{4,7},{5,6},{6,5},{7,4}} | collective-permute-start | bytes 10616840 | tf_op jit(solution)/shard_map/ppermute | solution.py:407
  83.2 68.0 %copy-start.8 = (f32[1152]{0:T(1024)S(1)}, f32[1152]{0:T(1024)}, u32[]{:S(2)}) copy-start(f32[1152]{0:T(1024)} %param.25) | copy-start | bytes 13828
  224.0 338.5 %collective-permute-start.6 = (bf16[2,256,1152]{2,1,0:T(8,128)(2,1)}, bf16[2,256,1152]{2,1,0:T(8,128)(2,1)}, u32[]{:S(2)}, u32[]{:S(2)}) collective-permute-start(bf16[2,256,1152]{2,1,0:T(8,128)(2,1)} %get-tuple-element.50), channel_id=1, source_target_pairs={{0,1},{1,0},{2,3},{3,2},{4,5},{5,4},{6,7},{7,6}} | collective-permute-start | bytes 3538952 | tf_op jit(solution)/shard_map/ppermute | solution.py:407
  224.3 340.1 %collective-permute-start.7 = (bf16[2,256,1152]{2,1,0:T(8,128)(2,1)}, bf16[2,256,1152]{2,1,0:T(8,128)(2,1)}, u32[]{:S(2)}, u32[]{:S(2)}) collective-permute-start(bf16[2,256,1152]{2,1,0:T(8,128)(2,1)} %get-tuple-element.51), channel_id=1, source_target_pairs={{0,2},{1,3},{2,0},{3,1},{4,6},{5,7},{6,4},{7,5}} | collective-permute-start | bytes 3538952 | tf_op jit(solution)/shard_map/ppermute | solution.py:407
  226.3 338.2 %collective-permute-start.8 = (bf16[2,256,1152]{2,1,0:T(8,128)(2,1)}, bf16[2,256,1152]{2,1,0:T(8,128)(2,1)}, u32[]{:S(2)}, u32[]{:S(2)}) collective-permute-start(bf16[2,256,1152]{2,1,0:T(8,128)(2,1)} %get-tuple-element.52), channel_id=1, source_target_pairs={{0,3},{1,2},{2,1},{3,0},{4,7},{5,6},{6,5},{7,4}} | collective-permute-start | bytes 3538952 | tf_op jit(solution)/shard_map/ppermute | solution.py:407
  562.0 4.2 collective-permute-start.12
  562.2 131.8 %collective-permute-start.9 = (bf16[3,256,1152]{2,1,0:T(8,128)(2,1)}, bf16[3,256,1152]{2,1,0:T(8,128)(2,1)}, u32[]{:S(2)}, u32[]{:S(2)}) collective-permute-start(bf16[3,256,1152]{2,1,0:T(8,128)(2,1)} %get-tuple-element.53), channel_id=1, source_target_pairs={{0,1},{1,0},{2,3},{3,2},{4,5},{5,4},{6,7},{7,6}} | collective-permute-start | bytes 5308424 | tf_op jit(solution)/shard_map/ppermute | solution.py:407
  562.5 131.5 %collective-permute-start.10 = (bf16[3,256,1152]{2,1,0:T(8,128)(2,1)}, bf16[3,256,1152]{2,1,0:T(8,128)(2,1)}, u32[]{:S(2)}, u32[]{:S(2)}) collective-permute-start(bf16[3,256,1152]{2,1,0:T(8,128)(2,1)} %get-tuple-element.54), channel_id=1, source_target_pairs={{0,2},{1,3},{2,0},{3,1},{4,6},{5,7},{6,4},{7,5}} | collective-permute-start | bytes 5308424 | tf_op jit(solution)/shard_map/ppermute | solution.py:407
  564.3 129.7 %collective-permute-start.11 = (bf16[3,256,1152]{2,1,0:T(8,128)(2,1)}, bf16[3,256,1152]{2,1,0:T(8,128)(2,1)}, u32[]{:S(2)}, u32[]{:S(2)}) collective-permute-start(bf16[3,256,1152]{2,1,0:T(8,128)(2,1)} %get-tuple-element.55), channel_id=1, source_target_pairs={{0,3},{1,2},{2,1},{3,0},{4,7},{5,6},{6,5},{7,4}} | collective-permute-start | bytes 5308424 | tf_op jit(solution)/shard_map/ppermute | solution.py:407
  564.4 103.1 %collective-permute-start.13 = (bf16[2,256,1152]{2,1,0:T(8,128)(2,1)}, bf16[2,256,1152]{2,1,0:T(8,128)(2,1)}, u32[]{:S(2)}, u32[]{:S(2)}) collective-permute-start(bf16[2,256,1152]{2,1,0:T(8,128)(2,1)} %get-tuple-element.57), channel_id=1, source_target_pairs={{0,2},{1,3},{2,0},{3,1},{4,6},{5,7},{6,4},{7,5}} | collective-permute-start | bytes 3538952 | tf_op jit(solution)/shard_map/ppermute | solution.py:407
  566.1 126.0 %collective-permute-start.14 = (bf16[2,256,1152]{2,1,0:T(8,128)(2,1)}, bf16[2,256,1152]{2,1,0:T(8,128)(2,1)}, u32[]{:S(2)}, u32[]{:S(2)}) collective-permute-start(bf16[2,256,1152]{2,1,0:T(8,128)(2,1)} %get-tuple-element.58), channel_id=1, source_target_pairs={{0,3},{1,2},{2,1},{3,0},{4,7},{5,6},{6,5},{7,4}} | collective-permute-start | bytes 3538952 | tf_op jit(solution)/shard_map/ppermute | solution.py:407
  667.5 52.1 %collective-permute-start.16 = (bf16[1,256,1152]{2,1,0:T(8,128)(2,1)}, bf16[1,256,1152]{2,1,0:T(8,128)(2,1)S(1)}, u32[]{:S(2)}, u32[]{:S(2)}) collective-permute-start(bf16[1,256,1152]{2,1,0:T(8,128)(2,1)} %get-tuple-element.48), channel_id=1, source_target_pairs={{0,2},{1,3},{2,0},{3,1},{4,6},{5,7},{6,4},{7,5}} | collective-permute-start | bytes 1769480 | tf_op jit(solution)/shard_map/ppermute | solution.py:407
  692.1 29.7 %copy-start.1 = (s32[4]{0:T(128)S(1)}, s32[4]{0:T(128)}, u32[]{:S(2)}) copy-start(s32[4]{0:T(128)} %pad_add_fusion.idx_ref.refs_11_.refs_0_) | copy-start | bytes 52
  692.1 27.5 %collective-permute-start.17 = (bf16[1,256,1152]{2,1,0:T(8,128)(2,1)}, bf16[1,256,1152]{2,1,0:T(8,128)(2,1)}, u32[]{:S(2)}, u32[]{:S(2)}) collective-permute-start(bf16[1,256,1152]{2,1,0:T(8,128)(2,1)} %get-tuple-element.61), channel_id=1, source_target_pairs={{0,3},{1,2},{2,1},{3,0},{4,7},{5,6},{6,5},{7,4}} | collective-permute-start | bytes 1769480 | tf_op jit(solution)/shard_map/ppermute | solution.py:407
  719.6 2.2 collective-permute-start.15
  (6 other events, 25.6 us)
